TPU v7x, 32 devices: a whole 2x2x4 slice. The times are simulated.
32 devices in a mesh: rep: 16 (over z, x, core), tp: 2 (over y).
Axes of the slice: x: 2, y: 2, z: 4, core: 2. Of those that a mesh axis runs over, the one named last changes fastest.
Arguments:
- tokens: bfloat16 [16, 256, 3072], P('rep', 'tp'), may hold values from -100 to 100
- norm_gain: float32 [16, 3072], P('rep'), may hold values from 0.5 to 1.5
- w_query: bfloat16 [16, 3072, 2048], P('rep', None, 'tp'), may hold values from -1 to 1
- key_weight: bfloat16 [16, 3072, 1024], P('rep', None, 'tp'), may hold values from -1 to 1
- value_weight: bfloat16 [16, 3072, 1024], P('rep', None, 'tp'), may hold values from -0.109375 to 0.109375
- attention_gradient: bfloat16 [16, 256, 2048], P('rep', None, 'tp'), may hold values from -6 to 6
- global_fragment: float32 [128, 3072], P('tp'), may hold values from -6 to 6
- momentum: float32 [128, 3072], P('tp'), may hold values from -3 to 3
- local_fragment: bfloat16 [16, 128, 3072], P('rep', 'tp'), may hold values from -6 to 6
Outputs:
- grad_query_w: bfloat16 [16, 3072, 2048], P('rep', None, 'tp')
- grad_key_w: bfloat16 [16, 3072, 1024], P('rep', None, 'tp')
- grad_value_w: bfloat16 [16, 3072, 1024], P('rep', None, 'tp')
- grad_gain: float32 [16, 3072], P('rep')
- grad_tokens: bfloat16 [16, 256, 3072], P('rep', 'tp')
- new_global: float32 [128, 3072], P('tp')
- new_momentum: float32 [128, 3072], P('tp')
All inputs are finite; a program needn't handle non-finite values.
Results may differ from a plain program's by a relative error of at most 0.019.
The roundings to bfloat16 on the way count: a program that leaves them out, or rounds other values in their place, can miss the bound.
Values may be sent and summed in bfloat16 or wider, within the bound.
A program may use at most 128 MiB of HBM per device.

v0:
```python
import jax
import jax.numpy as jnp
from jax import lax
from jax.sharding import PartitionSpec as P

HEAD_SIZE = 128
epsilon = 1e-05
rope_base = 500000.0
outer_rate = 0.7
outer_momentum = 0.9


def rope_tables(sequence_length, width):
    middle = width // 2
    frequency = rope_base ** (-2.0 * jnp.arange(middle, dtype=jnp.float32) / width)
    angles = jnp.arange(sequence_length, dtype=jnp.float32)[:, None] * frequency[None, :]
    angles = jnp.concatenate([angles, angles], axis=1)
    return (jnp.cos(angles)[:, None, :], jnp.sin(angles)[:, None, :])


def rotate(vectors, cosine_table, sine_table):
    middle = vectors.shape[-1] // 2
    turned = jnp.concatenate([-vectors[..., middle:], vectors[..., :middle]], axis=-1)
    return vectors * cosine_table + turned * sine_table


def reverse_rotation(gradient, cosine_table, sine_table):
    middle = gradient.shape[-1] // 2
    shifted = gradient * sine_table
    turned = jnp.concatenate([shifted[..., middle:], -shifted[..., :middle]], axis=-1)
    return gradient * cosine_table + turned


def attention_reverse(query_rows, rotated_keys, values_bfloat, grad_out, block_of_rows):
    sequence_length = query_rows.shape[0]
    score_scale = query_rows.shape[-1] ** (-0.5)

    def one_block(running, block_index):
        acc_key, acc_value = running
        offset = block_index * block_of_rows
        query_block = lax.dynamic_slice_in_dim(query_rows, offset, block_of_rows, 0)
        grad_block = lax.dynamic_slice_in_dim(grad_out, offset, block_of_rows, 0)
        scores = (
            jnp.einsum(
                "qgrd,kgd->grqk", query_block, rotated_keys, preferred_element_type=jnp.float32
            )
            * score_scale
        )
        row_pos = offset + jnp.arange(block_of_rows)
        col_pos = jnp.arange(sequence_length)
        allowed = col_pos[None, :] <= row_pos[:, None]
        scores = jnp.where(allowed, scores, -jnp.inf)
        highest = jnp.max(scores, axis=-1, keepdims=True)
        powers = jnp.exp(scores - highest)
        probability = powers / jnp.sum(powers, axis=-1, keepdims=True)
        prob_low = probability.astype(jnp.bfloat16)
        acc_value = acc_value + jnp.einsum(
            "grqk,qgrd->kgd", prob_low, grad_block, preferred_element_type=jnp.float32
        )
        grad_prob = jnp.einsum(
            "qgrd,kgd->grqk", grad_block, values_bfloat, preferred_element_type=jnp.float32
        )
        grad_score = (
            probability
            * (grad_prob - jnp.sum(grad_prob * probability, axis=-1, keepdims=True))
            * score_scale
        )
        score_low = grad_score.astype(jnp.bfloat16)
        grad_query = jnp.einsum(
            "grqk,kgd->qgrd", score_low, rotated_keys, preferred_element_type=jnp.float32
        )
        acc_key = acc_key + jnp.einsum(
            "grqk,qgrd->kgd", score_low, query_block, preferred_element_type=jnp.float32
        )
        return ((acc_key, acc_value), grad_query)

    initial = jnp.zeros(rotated_keys.shape, jnp.float32)
    (acc_key, acc_value), grad_blocks = lax.scan(
        one_block, (initial, initial), jnp.arange(sequence_length // block_of_rows)
    )
    return (grad_blocks.reshape(query_rows.shape), acc_key, acc_value)


def body(
    tokens,
    norm_gain,
    w_query,
    key_weight,
    value_weight,
    attention_gradient,
    global_fragment,
    momentum,
    local_fragment,
):
    local_rows = tokens[0]
    norm_gains = norm_gain[0]
    weight_q = w_query[0]
    weight_k = key_weight[0]
    weight_v = value_weight[0]
    widened_rows = local_rows.astype(jnp.float32)
    inverse_norm = lax.rsqrt(
        jnp.mean(widened_rows * widened_rows, axis=-1, keepdims=True) + epsilon
    )
    normalized_input = widened_rows * inverse_norm
    normalized_local = (normalized_input * norm_gains[None, :]).astype(jnp.bfloat16)
    normalized = lax.all_gather(normalized_local, "tp", axis=0, tiled=True)
    sequence_length = normalized.shape[0]
    heads_q = weight_q.shape[1] // HEAD_SIZE
    heads_kv = weight_k.shape[1] // HEAD_SIZE
    cosine_table, sine_table = rope_tables(sequence_length, HEAD_SIZE)
    query_rows = jnp.dot(normalized, weight_q, preferred_element_type=jnp.float32).reshape(
        sequence_length, heads_q, HEAD_SIZE
    )
    query_rows = rotate(query_rows, cosine_table, sine_table).astype(jnp.bfloat16)
    rotated_keys = jnp.dot(normalized, weight_k, preferred_element_type=jnp.float32).reshape(
        sequence_length, heads_kv, HEAD_SIZE
    )
    rotated_keys = rotate(rotated_keys, cosine_table, sine_table).astype(jnp.bfloat16)
    values_bfloat = (
        jnp.dot(normalized, weight_v, preferred_element_type=jnp.float32)
        .astype(jnp.bfloat16)
        .reshape(sequence_length, heads_kv, HEAD_SIZE)
    )
    replica_group = heads_q // heads_kv
    block_of_rows = min(512, sequence_length)
    query_input_gradient, key_input_gradient, value_input_gradient = attention_reverse(
        query_rows.reshape(sequence_length, heads_kv, replica_group, HEAD_SIZE),
        rotated_keys,
        values_bfloat,
        attention_gradient[0].reshape(sequence_length, heads_kv, replica_group, HEAD_SIZE),
        block_of_rows,
    )
    dquery = (
        reverse_rotation(
            query_input_gradient.reshape(sequence_length, heads_q, HEAD_SIZE),
            cosine_table,
            sine_table,
        )
        .astype(jnp.bfloat16)
        .reshape(sequence_length, heads_q * HEAD_SIZE)
    )
    key_gradient = (
        reverse_rotation(key_input_gradient, cosine_table, sine_table)
        .astype(jnp.bfloat16)
        .reshape(sequence_length, heads_kv * HEAD_SIZE)
    )
    value_gradient = value_input_gradient.astype(jnp.bfloat16).reshape(
        sequence_length, heads_kv * HEAD_SIZE
    )
    contract = (((0,), (0,)), ((), ()))
    grad_wq = lax.dot_general(
        normalized, dquery, contract, preferred_element_type=jnp.float32
    ).astype(jnp.bfloat16)
    grad_wk = lax.dot_general(
        normalized, key_gradient, contract, preferred_element_type=jnp.float32
    ).astype(jnp.bfloat16)
    grad_wv = lax.dot_general(
        normalized, value_gradient, contract, preferred_element_type=jnp.float32
    ).astype(jnp.bfloat16)
    back = (((1,), (1,)), ((), ()))
    partial_value = lax.dot_general(dquery, weight_q, back, preferred_element_type=jnp.float32)
    partial_value = partial_value + lax.dot_general(
        key_gradient, weight_k, back, preferred_element_type=jnp.float32
    )
    summed_rows = lax.psum_scatter(
        (
            partial_value
            + lax.dot_general(value_gradient, weight_v, back, preferred_element_type=jnp.float32)
        ).astype(jnp.bfloat16),
        "tp",
        scatter_dimension=0,
        tiled=True,
    ).astype(jnp.float32)
    gains_gradient = lax.psum(jnp.sum(summed_rows * normalized_input, axis=0), "tp")
    scaled_rows = summed_rows * norm_gains[None, :]
    gradient_rows = (
        inverse_norm
        * (
            scaled_rows
            - normalized_input * jnp.mean(scaled_rows * normalized_input, axis=-1, keepdims=True)
        )
    ).astype(jnp.bfloat16)
    delta = global_fragment - local_fragment[0].astype(jnp.float32)
    replicas = lax.axis_size("rep")
    mean_delta = lax.psum(delta, "rep") / replicas
    new_momentum = outer_momentum * momentum + mean_delta
    new_global = global_fragment - outer_rate * (mean_delta + outer_momentum * new_momentum)
    return (
        grad_wq[None],
        grad_wk[None],
        grad_wv[None],
        gains_gradient[None],
        gradient_rows[None],
        new_global,
        new_momentum,
    )


def solution(mesh):
    placed = (
        P("rep", "tp", None),
        P("rep", None),
        P("rep", None, "tp"),
        P("rep", None, "tp"),
        P("rep", None, "tp"),
        P("rep", None, "tp"),
        P("tp", None),
        P("tp", None),
        P("rep", "tp", None),
    )
    return jax.shard_map(
        body,
        mesh=mesh,
        in_specs=placed,
        out_specs=(
            P("rep", None, "tp"),
            P("rep", None, "tp"),
            P("rep", None, "tp"),
            P("rep", None),
            P("rep", "tp", None),
            P("tp", None),
            P("tp", None),
        ),
        check_vma=False,
    )
```

profile of v0, /device:TPU:0, one launch (start us, length us, event | category | flops | bytes accessed | tf_op | source)
XLA Modules:
  0.0 146.9 jit_solution(9005998716346742518)
XLA Ops:
  9.6 2.3 %fusion.22 = bf16[128,3072]{1,0:T(8,128)(2,1)} fusion(bf16[1,128,3072]{2,1,0:T(8,128)(2,1)} %param.9, f32[3072]{0:T(1024)} %bitcast.153, f32[128]{0:T(128)S(1)} %add_rsqrt_fusion), kind=kLoop, calls=%fused_computation.34 | loop fusion | flops 1572864 | bytes 1585664 | tf_op jit(solution)/shard_map/convert_element_type | solution.py:105
  12.0 2.1 %convert_subtract_fusion = f32[64,3072]{1,0:T(8,128)} fusion(f32[64,3072]{1,0:T(8,128)} %param.15, bf16[1,64,3072]{2,1,0:T(8,128)(2,1)S(1)} %copy-done.19), kind=kLoop, calls=%fused_computation.65 | loop fusion | flops 393216 | bytes 1966080 | tf_op jit(solution)/shard_map/sub | solution.py:183
  14.2 8.7 %copy.38 = bf16[1024,3072]{1,0:T(8,128)(2,1)} copy(bf16[1024,3072]{0,1:T(8,128)(2,1)} %bitcast.138) | data formatting | bytes 12582912 | tf_op jit(solution)/shard_map/dot_general | solution.py:111
  23.4 4.7 %copy.35 = bf16[512,3072]{1,0:T(8,128)(2,1)} copy(bf16[512,3072]{0,1:T(8,128)(2,1)} %bitcast.137) | data formatting | bytes 6291456 | tf_op jit(solution)/shard_map/dot_general | solution.py:115
  28.1 2.0 %copy.41 = bf16[1,256,1024]{1,2,0:T(8,128)(2,1)} copy(bf16[1,256,1024]{2,1,0:T(8,128)(2,1)} %param.14) | data formatting | bytes 1048576 | tf_op jit(solution)/shard_map/reshape;squeeze | solution.py:130
  30.2 11.8 %all-gather.2.cloned.1.call-done = bf16[256,3072]{1,0:T(8,128)(2,1)} async-done(((bf16[128,3072]{1,0:T(8,128)(2,1)}), bf16[256,3072]{1,0:T(8,128)(2,1)}) %all-gather.2.cloned.1.call-update) | async-done | bytes 1572880 | tf_op jit(solution)/shard_map/all_gather | solution.py:106
  42.0 5.3 %fusion.26 = f32[256,8,128]{0,2,1:T(8,128)S(1)} fusion(bf16[8,128,3072]{2,1,0:T(8,128)(2,1)} %bitcast.141, bf16[256,3072]{1,0:T(8,128)(2,1)} %all-gather.2.cloned.1.call-done), kind=kOutput, calls=%fused_computation.38 | convolution fusion | flops 1610612736 | bytes 8912896 | tf_op jit(solution)/shard_map/dot_general | solution.py:111
  51.5 1.7 %fusion.30 = bf16[256,512]{1,0:T(8,128)(2,1)} fusion(bf16[256,3072]{1,0:T(8,128)(2,1)S(1)} %copy-done.1, bf16[1,3072,512]{2,1,0:T(8,128)(2,1)S(1)} %copy-done), kind=kOutput, calls=%fused_computation.44 | convolution fusion | flops 805437440 | bytes 4980736 | tf_op jit(solution)/shard_map/dot_general | solution.py:120
  55.0 2.7 %fusion.35 = bf16[256,8,128]{0,2,1:T(8,128)(2,1)} fusion(f32[256,8,64]{0,2,1:T(8,128)} %get-tuple-element.40, f32[256,8,64]{0,2,1:T(8,128)} %get-tuple-element.39, f32[256,8,128]{0,2,1:T(8,128)} %copy-done.7, f32[256,128]{0,1:T(8,128)S(1)} %get-tuple-element.46, f32[256,128]{0,1:T(8,128)S(1)} %get-tuple-element.45), kind=kLoop, calls=%fused_computation.48 | loop fusion | flops 1310720 | bytes 2883584 | tf_op jit(solution)/shard_map/convert_element_type | solution.py:114
  58.5 1.7 %fusion.51 = f32[4,256,256,2]{2,1,3,0:T(8,128)} fusion(bf16[256,4,2,128]{0,3,2,1:T(8,128)(2,1)S(1)} %bitcast.146, bf16[256,4,128,1]{2,1,0,3:T(4,128)(2,1)S(1)} %bitcast.149), kind=kOutput, calls=%fused_computation.78 | convolution fusion | flops 134217728 | bytes 2883584 | tf_op jit(solution)/shard_map/while/body/eval_jaxpr/qgrd,kgd->grqk/dot_general | solution.py:60
  60.2 3.3 %fusion.65 = (f32[4,2,256]{2,1,0:T(2,128)S(1)}, f32[4,2,256,256]{2,3,1,0:T(8,128)}) fusion(pred[256,256]{0,1:T(8,128)(4,1)S(1)} %iota_compare_fusion, bf16[256,4,128,1]{0,2,3,1:T(8,128)(2,1)} %fusion.50, bf16[256,4,2,128]{0,3,2,1:T(8,128)(2,1)} %bitcast.150), kind=kOutput, calls=%fused_computation.98 | convolution fusion | flops 136315136 | bytes 2957312 | tf_op jit(solution)/shard_map/while/body/eval_jaxpr/sub | solution.py:54
  63.5 5.4 %broadcast_multiply_fusion = (f32[256,4,128]{0,2,1:T(8,128)}, f32[256,4,128]{0,2,1:T(8,128)}) fusion(f32[256,128]{0,1:T(8,128)S(1)} %get-tuple-element.46, bf16[256,4,2,128]{0,3,2,1:T(8,128)(2,1)} %bitcast.151, f32[4,256,256,2]{2,1,3,0:T(8,128)} %fusion.51, f32[4,2,256,256]{2,3,1,0:T(8,128)} %get-tuple-element.48, f32[4,2,256]{2,1,0:T(2,128)S(1)} %get-tuple-element.47), kind=kOutput, calls=%fused_computation.81 | convolution fusion | flops 138021120 | bytes 5906432 | tf_op jit(solution)/shard_map/while/body/eval_jaxpr/grqk,qgrd->kgd/dot_general | solution.py:72
  68.8 5.3 %fusion.44 = f32[4,128,2,256]{3,1,2,0:T(8,128)} fusion(bf16[256,4,128,1]{0,2,3,1:T(8,128)(2,1)} %fusion.50, f32[4,256,256,2]{2,1,3,0:T(8,128)} %fusion.51, f32[4,2,256,256]{2,3,1,0:T(8,128)} %get-tuple-element.48, f32[4,2,256]{2,1,0:T(2,128)S(1)} %get-tuple-element.47), kind=kOutput, calls=%fused_computation.62 | convolution fusion | flops 137890048 | bytes 5513216 | tf_op jit(solution)/shard_map/while/body/eval_jaxpr/grqk,kgd->qgrd/dot_general | solution.py:69
  74.2 2.3 %fusion.33 = bf16[4,256,128]{1,2,0:T(8,128)(2,1)S(1)} fusion(bf16[256,4,2,128]{0,3,2,1:T(8,128)(2,1)} %bitcast.145, f32[4,2,256,256]{2,3,1,0:T(8,128)} %get-tuple-element.48, f32[4,2,256]{2,1,0:T(2,128)S(1)} %get-tuple-element.47), kind=kOutput, calls=%fused_computation.45 | convolution fusion | flops 135397376 | bytes 2891776 | tf_op jit(solution)/shard_map/while/body/eval_jaxpr/grqk,qgrd->kgd/dot_general | solution.py:57
  79.0 1.8 %fusion.2 = f32[256,3072]{1,0:T(8,128)S(1)} fusion(bf16[256,1024]{0,1:T(8,128)(2,1)S(1)} %bitcast.152, bf16[1,3072,1024]{2,1,0:T(8,128)(2,1)S(1)} %bitcast.140), kind=kOutput, calls=%fused_computation.2 | convolution fusion | flops 1610612736 | bytes 9961472 | tf_op jit(solution)/shard_map/dot_general | solution.py:161
  82.1 2.2 %fusion.6 = bf16[256,3072]{1,0:T(8,128)(2,1)} fusion(f32[256,3072]{1,0:T(8,128)S(1)} %convolution_add_fusion.1, bf16[256,512]{0,1:T(8,128)(2,1)S(1)} %bitcast.147, bf16[1,3072,512]{2,1,0:T(8,128)(2,1)S(1)} %copy-done), kind=kOutput, calls=%fused_computation.11 | convolution fusion | flops 806879232 | bytes 8126464 | tf_op jit(solution)/shard_map/dot_general | solution.py:168
  84.3 27.0 %all-reduce.2.cloned.1.call-done = f32[64,3072]{1,0:T(8,128)} async-done(((f32[64,3072]{1,0:T(8,128)}), f32[64,3072]{1,0:T(8,128)}) %all-reduce.2.cloned.1.call-update) | async-done | bytes 786448 | tf_op jit(solution)/shard_map/psum | solution.py:185
  111.3 3.1 %multiply_subtract_fusion = (f32[64,3072]{1,0:T(8,128)}, f32[64,3072]{1,0:T(8,128)}) fusion(f32[64,3072]{1,0:T(8,128)} %param.15, f32[64,3072]{1,0:T(8,128)} %all-reduce.2.cloned.1.call-done, f32[64,3072]{1,0:T(8,128)} %param.16), kind=kLoop, calls=%fused_computation.66 | loop fusion | flops 1376256 | bytes 3932160 | tf_op jit(solution)/shard_map/sub | solution.py:187
  115.9 2.9 %fusion.5 = bf16[1,3072,512]{2,1,0:T(8,128)(2,1)} fusion(bf16[256,3072]{1,0:T(8,128)(2,1)S(1)} %copy-done.2, bf16[256,512]{0,1:T(8,128)(2,1)S(1)} %bitcast.148), kind=kOutput, calls=%fused_computation.8 | convolution fusion | flops 806879232 | bytes 4980736 | tf_op jit(solution)/shard_map/dot_general | solution.py:157
  118.8 2.7 %fusion.4 = bf16[1,3072,512]{2,1,0:T(8,128)(2,1)} fusion(bf16[256,3072]{1,0:T(8,128)(2,1)S(1)} %copy-done.2, bf16[256,512]{0,1:T(8,128)(2,1)S(1)} %bitcast.144), kind=kOutput, calls=%fused_computation.7 | convolution fusion | flops 806879232 | bytes 4980736 | tf_op jit(solution)/shard_map/dot_general | solution.py:154
  121.5 4.6 %convert_bitcast_fusion = bf16[1,3072,1024]{2,1,0:T(8,128)(2,1)} fusion(bf16[256,3072]{1,0:T(8,128)(2,1)S(1)} %copy-done.2, bf16[256,1024]{0,1:T(8,128)(2,1)S(1)} %fusion.37), kind=kOutput, calls=%fused_computation.4 | convolution fusion | flops 1613758464 | bytes 8388608 | tf_op jit(solution)/shard_map/dot_general | solution.py:151
  126.1 1.9 %fusion.24 = (f32[128]{0:T(128)S(1)}, f32[3072]{0:T(1024)S(1)}) fusion(bf16[128,3072]{1,0:T(8,128)(2,1)} %reduce-scatter.2.cloned.1.call-done, bf16[1,128,3072]{2,1,0:T(8,128)(2,1)} %param.9, f32[3072]{0:T(1024)S(1)} %bitcast.154, f32[128]{0:T(128)S(1)} %add_rsqrt_fusion), kind=kLoop, calls=%fused_computation.36 | loop fusion | flops 3142528 | bytes 1598464 | tf_op jit(solution)/shard_map/reduce_sum | solution.py:180
  128.0 8.8 %psum.14 = f32[1,3072]{1,0:T(1,128)} all-reduce(f32[1,3072]{1,0:T(1,128)S(1)} %bitcast.156), channel_id=1, replica_groups=mesh['rep'=16,'tp'=2] {'tp'}, use_global_device_ids=true, to_apply=%region_6.7 | all-reduce | flops 3072 | bytes 24576 | tf_op jit(solution)/shard_map/psum | solution.py:174
  136.8 2.7 %fusion.46 = bf16[1,128,3072]{2,1,0:T(8,128)(2,1)} fusion(bf16[128,3072]{1,0:T(8,128)(2,1)} %reduce-scatter.2.cloned.1.call-done, bf16[1,128,3072]{2,1,0:T(8,128)(2,1)} %param.9, f32[128]{0:T(128)S(1)} %broadcast_multiply_fusion.1, f32[3072]{0:T(1024)S(1)} %bitcast.155, f32[128]{0:T(128)S(1)} %add_rsqrt_fusion), kind=kLoop, calls=%fused_computation.64 | loop fusion | flops 3145728 | bytes 2372608 | tf_op jit(solution)/shard_map/broadcast_in_dim | solution.py:193
  (73 shorter events, 14.2 us)
Async XLA Ops:
  8.0 43.5 %copy-start = (bf16[1,3072,512]{2,1,0:T(8,128)(2,1)S(1)}, bf16[1,3072,512]{2,1,0:T(8,128)(2,1)}, u32[]{:S(2)}) copy-start(bf16[1,3072,512]{2,1,0:T(8,128)(2,1)} %param.13) | copy-start | bytes 9437188
  8.0 4.0 %copy-start.19 = (bf16[1,64,3072]{2,1,0:T(8,128)(2,1)S(1)}, bf16[1,64,3072]{2,1,0:T(8,128)(2,1)}, u32[]{:S(2)}) copy-start(bf16[1,64,3072]{2,1,0:T(8,128)(2,1)} %param.17) | copy-start | bytes 1179652
  8.0 34.0 %all-gather.2.cloned.1.call-start = ((), (), s32[]{:S(2)}) async-start(), calls=%async_computation.1 | async-start | bytes 2359296 | tf_op jit(solution)/shard_map/all_gather | solution.py:106
  11.9 99.4 %all-reduce.2.cloned.1.call-start = ((), (), s32[]{:S(2)}) async-start(), calls=%async_computation.3 | async-start | bytes 1572864 | tf_op jit(solution)/shard_map/psum | solution.py:185
  14.1 112.0 %reduce-scatter.2.cloned.1.call-start = ((), (), s32[]{:S(2)}) async-start(), calls=%async_computation.2 | async-start | bytes 2359296 | tf_op jit(solution)/shard_map/reduce_scatter | solution.py:165
  42.0 6.4 %copy-start.8 = (bf16[512,3072]{1,0:T(8,128)(2,1)S(1)}, bf16[512,3072]{1,0:T(8,128)(2,1)}, u32[]{:S(2)}) copy-start(bf16[512,3072]{1,0:T(8,128)(2,1)} %copy.35) | copy-start | bytes 9437188
  47.3 3.2 %copy-start.7 = (f32[256,8,128]{0,2,1:T(8,128)}, f32[256,8,128]{0,2,1:T(8,128)S(1)}, u32[]{:S(2)}) copy-start(f32[256,8,128]{0,2,1:T(8,128)S(1)} %fusion.26) | copy-start | bytes 3145732
  47.3 2.2 %copy-start.1 = (bf16[256,3072]{1,0:T(8,128)(2,1)S(1)}, bf16[256,3072]{1,0:T(8,128)(2,1)}, u32[]{:S(2)}) copy-start(bf16[256,3072]{1,0:T(8,128)(2,1)} %all-gather.2.cloned.1.call-done) | copy-start | bytes 4718596
  55.0 2.7 %copy-start.10 = (f32[256,4,128]{0,2,1:T(8,128)S(1)}, f32[256,4,128]{0,2,1:T(8,128)}, u32[]{:S(2)}) copy-start(f32[256,4,128]{0,2,1:T(8,128)} %copy-done.9) | copy-start | bytes 1572868
  55.0 2.7 %copy-start.14 = (f32[256,4,64]{0,2,1:T(8,128)S(1)}, f32[256,4,64]{0,2,1:T(8,128)}, u32[]{:S(2)}) copy-start(f32[256,4,64]{0,2,1:T(8,128)} %get-tuple-element.43) | copy-start | bytes 786436
  55.0 2.7 %copy-start.15 = (f32[256,4,64]{0,2,1:T(8,128)S(1)}, f32[256,4,64]{0,2,1:T(8,128)}, u32[]{:S(2)}) copy-start(f32[256,4,64]{0,2,1:T(8,128)} %get-tuple-element.44) | copy-start | bytes 786436
  55.0 3.5 %copy-start.11 = (bf16[1,256,1024]{1,2,0:T(8,128)(2,1)S(1)}, bf16[1,256,1024]{1,2,0:T(8,128)(2,1)}, u32[]{:S(2)}) copy-start(bf16[1,256,1024]{1,2,0:T(8,128)(2,1)} %copy.41) | copy-start | bytes 1572868
  55.0 3.5 %copy-start.16 = (bf16[256,4,128]{2,1,0:T(4,128)(2,1)S(1)}, bf16[256,4,128]{2,1,0:T(4,128)(2,1)}, u32[]{:S(2)}) copy-start(bf16[256,4,128]{2,1,0:T(4,128)(2,1)} %reshape.115) | copy-start | bytes 786436
  74.2 2.3 %copy-start.17 = (f32[256,4,128]{0,2,1:T(8,128)S(1)}, f32[256,4,128]{0,2,1:T(8,128)}, u32[]{:S(2)}) copy-start(f32[256,4,128]{0,2,1:T(8,128)} %get-tuple-element.49) | copy-start | bytes 1572868
  74.2 2.4 %copy-start.4 = (f32[4,128,2,256]{3,1,2,0:T(8,128)S(1)}, f32[4,128,2,256]{3,1,2,0:T(8,128)}, u32[]{:S(2)}) copy-start(f32[4,128,2,256]{3,1,2,0:T(8,128)} %fusion.44) | copy-start | bytes 3145732
  74.2 3.7 %slice-start = ((s8[6291456]{0:T(1024)(128)(4,1)}), s8[4194304]{0:T(1024)(128)(4,1)S(1)}, s32[]{:S(2)}) async-start(s8[6291456]{0:T(1024)(128)(4,1)} %bitcast.139), calls=%async_computation.4 | async-start | bytes 8388608
  76.5 5.6 %copy-start.12 = (bf16[4,256,128]{1,2,0:T(8,128)(2,1)}, bf16[4,256,128]{1,2,0:T(8,128)(2,1)S(1)}, u32[]{:S(2)}) copy-start(bf16[4,256,128]{1,2,0:T(8,128)(2,1)S(1)} %fusion.33) | copy-start | bytes 786436
  76.5 2.5 %slice-start.1 = ((s8[6291456]{0:T(1024)(128)(4,1)}), s8[2097152]{0:T(1024)(128)(4,1)S(1)}, s32[]{:S(2)}) async-start(s8[6291456]{0:T(1024)(128)(4,1)} %bitcast.139), calls=%async_computation.5 | async-start | bytes 4194304
  79.0 1.9 %copy-start.18 = (f32[256,4,128]{0,2,1:T(8,128)S(1)}, f32[256,4,128]{0,2,1:T(8,128)}, u32[]{:S(2)}) copy-start(f32[256,4,128]{0,2,1:T(8,128)} %get-tuple-element.50) | copy-start | bytes 1572868
  79.0 2.1 %copy-start.3 = (bf16[1,3072,512]{2,1,0:T(8,128)(2,1)S(1)}, bf16[1,3072,512]{2,1,0:T(8,128)(2,1)}, u32[]{:S(2)}) copy-start(bf16[1,3072,512]{2,1,0:T(8,128)(2,1)} %param.12) | copy-start | bytes 9437188
  111.3 3.1 %copy-start.5 = (f32[4,128,2,256]{3,1,2,0:T(8,128)S(1)}, f32[4,128,2,256]{3,1,2,0:T(8,128)}, u32[]{:S(2)}) copy-start(f32[4,128,2,256]{3,1,2,0:T(8,128)} %fusion.44) | copy-start | bytes 3145732
  111.3 3.1 %copy-start.6 = (f32[256,8,128]{0,2,1:T(8,128)S(1)}, f32[256,8,128]{0,2,1:T(8,128)}, u32[]{:S(2)}) copy-start(f32[256,8,128]{0,2,1:T(8,128)} %get-tuple-element.36) | copy-start | bytes 3145732
  114.5 1.4 copy-start.13
  121.5 4.6 %copy-start.20 = (f32[1,3072]{1,0:T(1,128)S(1)}, f32[1,3072]{1,0:T(1,128)}, u32[]{:S(2)}) copy-start(f32[1,3072]{1,0:T(1,128)} %param.10) | copy-start | bytes 36868
  (2 other events, 2.4 us)
Sparse Core Ops, SparseCore 0:
  12.1 29.9 all-gather.1
  84.5 26.1 reduce-scatter.1
Sparse Core Ops, SparseCore 1:
  16.4 94.9 all-reduce.1
where the time goes:
time: 148 us; the launch traced here: 147 us
  matrix products  41.3 us (28%)
  waiting for transfers between devices  38.9 us (26%)
  other arithmetic  21.3 us (14%)
  local copies, waits for them, and re-layouts  20.8 us (14%)
  between operations  15.7 us (11%)
  blocking collectives  8.76 us (6%)
    psum x1, waiting for transfers between devices, body(): mean_delta = lax.psum(delta, 'rep') / replicas  27 us
    all_gather x1, waiting for transfers between devices, body(): normalized = lax.all_gather(normalized_local, 'tp', axis=0, tiled=True)  11.8 us
    psum x1, blocking collectives, body(): lax.psum(jnp.sum(summed_rows * normalized_input, axis=0), 'tp')  8.76 us
    dot_general x1, local copies, waits for them, and re-layouts, body(): jnp.dot(normalized, weight_q, preferred_element_type=jnp.float32)  8.68 us
    dot_general x1, matrix products, one_block(): jnp.einsum('grqk,qgrd->kgd', score_low, query_block, preferred_element_ty...  5.36 us
    dot_general x1, matrix products, one_block(): jnp.einsum('grqk,kgd->qgrd', score_low, rotated_keys, preferred_element_t...  5.3 us
    dot_general x1, matrix products, body(): jnp.dot(normalized, weight_q, preferred_element_type=jnp.float32)  5.26 us
    dot_general x1, local copies, waits for them, and re-layouts, body(): jnp.dot(normalized, weight_k, preferred_element_type=jnp.float32)  4.69 us
  transfers between devices with their start and end apart: 3, of which 2 were waited for; matrix products, arithmetic and copies ran while one was open for 49% of the time, Pallas kernels for 0%

commit v1 on v0

--- a/solution.py
+++ b/solution.py
@@ -182,7 +182,7 @@
     ).astype(jnp.bfloat16)
     delta = global_fragment - local_fragment[0].astype(jnp.float32)
     replicas = lax.axis_size("rep")
-    mean_delta = lax.psum(delta, "rep") / replicas
+    mean_delta = jnp.sum(lax.all_gather(delta, "rep"), axis=0) / replicas
     new_momentum = outer_momentum * momentum + mean_delta
     new_global = global_fragment - outer_rate * (mean_delta + outer_momentum * new_momentum)
     return (

time: 148 us -> 210 us (1.42)
  waiting for transfers between devices: 38.9 us -> 91.1 us
  other arithmetic: 21.3 us -> 28 us
  matrix products: 41.3 us -> 47.8 us
  local copies, waits for them, and re-layouts: 20.8 us -> 18.4 us
    all_gather x0 -> x1, waiting for transfers between devices: none -> 65.1 us  [body(): mean_delta = jnp.sum(lax.all_gather(delta, 'rep'), axis=0) / replicas]
    psum x1 -> x0, waiting for transfers between devices: 27 us -> none  [body(): mean_delta = lax.psum(delta, 'rep') / replicas]
    reduce_scatter x1, waiting for transfers between devices: 0.01 us -> 11.8 us  [body(): lax.psum_scatter((partial_value + lax.dot_general(value_gradient, weight_...]
    reduce_sum x0 -> x1, other arithmetic: none -> 6.27 us  [body(): mean_delta = jnp.sum(lax.all_gather(delta, 'rep'), axis=0) / replicas]
    dot_general x1, matrix products: 1.84 us -> 4.85 us  [body(): lax.dot_general(dquery, weight_q, back, preferred_element_type=jnp.float32)]
    dot_general x1, matrix products: 1.05 us -> 3.49 us  [body(): jnp.dot(normalized, weight_k, preferred_element_type=jnp.float32)]
    unnamed x46 -> x22, local copies, waits for them, and re-layouts: 3.6 us -> 1.3 us
    all_gather x1, waiting for transfers between devices: 11.8 us -> 14.1 us  [body(): normalized = lax.all_gather(normalized_local, 'tp', axis=0, tiled=True)]
  transfers between devices with their start and end apart: 3 -> 3, of which waited for: 2 -> 3; matrix products, arithmetic and copies ran while one was open for 49% -> 17% of each run, Pallas kernels for 0% -> 0%
where the time goes in v1:
time: 210 us; the launch traced here: 209 us
  waiting for transfers between devices  91.1 us (43%)
  matrix products  47.8 us (23%)
  other arithmetic  28 us (13%)
  local copies, waits for them, and re-layouts  18.4 us (9%)
  between operations  15.7 us (7%)
  blocking collectives  7.54 us (4%)
    all_gather x1, waiting for transfers between devices, body(): mean_delta = jnp.sum(lax.all_gather(delta, 'rep'), axis=0) / replicas  65.1 us
    all_gather x1, waiting for transfers between devices, body(): normalized = lax.all_gather(normalized_local, 'tp', axis=0, tiled=True)  14.1 us
    reduce_scatter x1, waiting for transfers between devices, body(): lax.psum_scatter((partial_value + lax.dot_general(value_gradient, weight_...  11.8 us
    dot_general x1, local copies, waits for them, and re-layouts, body(): jnp.dot(normalized, weight_q, preferred_element_type=jnp.float32)  8.68 us
    psum x1, blocking collectives, body(): lax.psum(jnp.sum(summed_rows * normalized_input, axis=0), 'tp')  7.54 us
    reduce_sum x1, other arithmetic, body(): mean_delta = jnp.sum(lax.all_gather(delta, 'rep'), axis=0) / replicas  6.27 us
    dot_general x1, matrix products, one_block(): jnp.einsum('grqk,qgrd->kgd', score_low, query_block, preferred_element_ty...  5.35 us
    dot_general x1, matrix products, one_block(): jnp.einsum('grqk,kgd->qgrd', score_low, rotated_keys, preferred_element_t...  5.26 us
  transfers between devices with their start and end apart: 3, of which 3 were waited for; matrix products, arithmetic and copies ran while one was open for 17% of the time, Pallas kernels for 0%

profile of v1, /device:TPU:0, one launch (start us, length us, event | category | flops | bytes accessed | tf_op | source)
XLA Modules:
  0.0 208.7 jit_solution(5767906690166812729)
XLA Ops:
  9.6 2.3 %fusion.22 = bf16[128,3072]{1,0:T(8,128)(2,1)} fusion(bf16[1,128,3072]{2,1,0:T(8,128)(2,1)} %param.9, f32[3072]{0:T(1024)} %bitcast.153, f32[128]{0:T(128)S(1)} %add_rsqrt_fusion), kind=kLoop, calls=%fused_computation.34 | loop fusion | flops 1572864 | bytes 1585664 | tf_op jit(solution)/shard_map/convert_element_type | solution.py:105
  12.0 2.0 copy.41
  14.0 4.6 %copy.35 = bf16[512,3072]{1,0:T(8,128)(2,1)} copy(bf16[512,3072]{0,1:T(8,128)(2,1)} %bitcast.139) | data formatting | bytes 6291456 | tf_op jit(solution)/shard_map/dot_general | solution.py:115
  18.6 8.7 %copy.38 = bf16[1024,3072]{1,0:T(8,128)(2,1)} copy(bf16[1024,3072]{0,1:T(8,128)(2,1)} %bitcast.140) | data formatting | bytes 12582912 | tf_op jit(solution)/shard_map/dot_general | solution.py:111
  27.9 14.1 %all-gather.4.cloned.1.call-done = bf16[256,3072]{1,0:T(8,128)(2,1)} async-done(((bf16[128,3072]{1,0:T(8,128)(2,1)}), bf16[256,3072]{1,0:T(8,128)(2,1)}) %all-gather.4.cloned.1.call-update) | async-done | bytes 1572880 | tf_op jit(solution)/shard_map/all_gather | solution.py:106
  42.0 3.1 %fusion.30 = bf16[256,512]{1,0:T(8,128)(2,1)} fusion(bf16[256,3072]{1,0:T(8,128)(2,1)} %all-gather.4.cloned.1.call-done, bf16[1,3072,512]{2,1,0:T(8,128)(2,1)S(1)} %copy-done), kind=kOutput, calls=%fused_computation.44 | convolution fusion | flops 805437440 | bytes 4980736 | tf_op jit(solution)/shard_map/dot_general | solution.py:120
  46.8 3.5 %fusion.28 = f32[256,4,128]{0,2,1:T(8,128)S(1)} fusion(bf16[4,128,3072]{2,1,0:T(8,128)(2,1)} %bitcast.142, bf16[256,3072]{1,0:T(8,128)(2,1)} %all-gather.4.cloned.1.call-done), kind=kOutput, calls=%fused_computation.40 | convolution fusion | flops 805306368 | bytes 5242880 | tf_op jit(solution)/shard_map/dot_general | solution.py:115
  50.3 4.6 %fusion.26 = f32[256,8,128]{0,2,1:T(8,128)S(1)} fusion(bf16[8,128,3072]{2,1,0:T(8,128)(2,1)} %bitcast.141, bf16[256,3072]{1,0:T(8,128)(2,1)S(1)} %copy-done.1), kind=kOutput, calls=%fused_computation.38 | convolution fusion | flops 1610612736 | bytes 8912896 | tf_op jit(solution)/shard_map/dot_general | solution.py:111
  59.6 3.3 %fusion.65 = (f32[4,2,256]{2,1,0:T(2,128)S(1)}, f32[4,2,256,256]{2,3,1,0:T(8,128)}) fusion(pred[256,256]{0,1:T(8,128)(4,1)S(1)} %iota_compare_fusion, bf16[256,4,128,1]{0,2,3,1:T(8,128)(2,1)} %fusion.50, bf16[256,4,2,128]{0,3,2,1:T(8,128)(2,1)} %bitcast.150), kind=kOutput, calls=%fused_computation.98 | convolution fusion | flops 136315136 | bytes 2957312 | tf_op jit(solution)/shard_map/while/body/eval_jaxpr/sub | solution.py:54
  62.9 2.9 %fusion.33 = bf16[4,256,128]{1,2,0:T(8,128)(2,1)} fusion(bf16[256,4,2,128]{0,3,2,1:T(8,128)(2,1)} %bitcast.145, f32[4,2,256,256]{2,3,1,0:T(8,128)} %get-tuple-element.48, f32[4,2,256]{2,1,0:T(2,128)S(1)} %get-tuple-element.47), kind=kOutput, calls=%fused_computation.45 | convolution fusion | flops 135397376 | bytes 2891776 | tf_op jit(solution)/shard_map/while/body/eval_jaxpr/grqk,qgrd->kgd/dot_general | solution.py:57
  65.8 5.4 %broadcast_multiply_fusion = (f32[256,4,128]{0,2,1:T(8,128)}, f32[256,4,128]{0,2,1:T(8,128)}) fusion(f32[256,128]{0,1:T(8,128)S(1)} %get-tuple-element.46, bf16[256,4,2,128]{0,3,2,1:T(8,128)(2,1)} %bitcast.151, f32[4,256,256,2]{2,1,3,0:T(8,128)} %fusion.51, f32[4,2,256,256]{2,3,1,0:T(8,128)} %get-tuple-element.48, f32[4,2,256]{2,1,0:T(2,128)S(1)} %get-tuple-element.47), kind=kOutput, calls=%fused_computation.81 | convolution fusion | flops 138021120 | bytes 5906432 | tf_op jit(solution)/shard_map/while/body/eval_jaxpr/grqk,qgrd->kgd/dot_general | solution.py:72
  71.1 5.3 %fusion.44 = f32[4,128,2,256]{3,1,2,0:T(8,128)} fusion(bf16[256,4,128,1]{0,2,3,1:T(8,128)(2,1)} %fusion.50, f32[4,256,256,2]{2,1,3,0:T(8,128)} %fusion.51, f32[4,2,256,256]{2,3,1,0:T(8,128)} %get-tuple-element.48, f32[4,2,256]{2,1,0:T(2,128)S(1)} %get-tuple-element.47), kind=kOutput, calls=%fused_computation.62 | convolution fusion | flops 137890048 | bytes 5513216 | tf_op jit(solution)/shard_map/while/body/eval_jaxpr/grqk,kgd->qgrd/dot_general | solution.py:69
  80.2 4.8 %fusion.2 = f32[256,3072]{1,0:T(8,128)S(1)} fusion(bf16[256,1024]{0,1:T(8,128)(2,1)S(1)} %bitcast.152, bf16[1,3072,1024]{2,1,0:T(8,128)(2,1)} %param.11), kind=kOutput, calls=%fused_computation.2 | convolution fusion | flops 1610612736 | bytes 9961472 | tf_op jit(solution)/shard_map/dot_general | solution.py:161
  86.2 2.2 %fusion.6 = bf16[256,3072]{1,0:T(8,128)(2,1)} fusion(f32[256,3072]{1,0:T(8,128)S(1)} %convolution_add_fusion.1, bf16[256,512]{0,1:T(8,128)(2,1)S(1)} %bitcast.147, bf16[1,3072,512]{2,1,0:T(8,128)(2,1)S(1)} %copy-done), kind=kOutput, calls=%fused_computation.11 | convolution fusion | flops 806879232 | bytes 8126464 | tf_op jit(solution)/shard_map/dot_general | solution.py:168
  88.7 2.2 %convert_subtract_fusion = f32[64,3072]{1,0:T(8,128)} fusion(f32[64,3072]{1,0:T(8,128)} %param.15, bf16[1,64,3072]{2,1,0:T(8,128)(2,1)} %param.17), kind=kLoop, calls=%fused_computation.65 | loop fusion | flops 393216 | bytes 1966080 | tf_op jit(solution)/shard_map/sub | solution.py:183
  92.9 2.7 %fusion.5 = bf16[1,3072,512]{2,1,0:T(8,128)(2,1)} fusion(bf16[256,3072]{1,0:T(8,128)(2,1)S(1)} %copy-done.2, bf16[256,512]{0,1:T(8,128)(2,1)S(1)} %bitcast.148), kind=kOutput, calls=%fused_computation.8 | convolution fusion | flops 806879232 | bytes 4980736 | tf_op jit(solution)/shard_map/dot_general | solution.py:157
  95.6 2.7 %fusion.4 = bf16[1,3072,512]{2,1,0:T(8,128)(2,1)} fusion(bf16[256,3072]{1,0:T(8,128)(2,1)S(1)} %copy-done.2, bf16[256,512]{0,1:T(8,128)(2,1)S(1)} %bitcast.144), kind=kOutput, calls=%fused_computation.7 | convolution fusion | flops 806879232 | bytes 4980736 | tf_op jit(solution)/shard_map/dot_general | solution.py:154
  98.3 4.6 %convert_bitcast_fusion = bf16[1,3072,1024]{2,1,0:T(8,128)(2,1)} fusion(bf16[256,3072]{1,0:T(8,128)(2,1)S(1)} %copy-done.2, bf16[256,1024]{0,1:T(8,128)(2,1)S(1)} %fusion.37), kind=kOutput, calls=%fused_computation.4 | convolution fusion | flops 1613758464 | bytes 8388608 | tf_op jit(solution)/shard_map/dot_general | solution.py:151
  102.9 11.8 %reduce-scatter.2.cloned.1.call-done = bf16[128,3072]{1,0:T(8,128)(2,1)} async-done(((bf16[256,3072]{1,0:T(8,128)(2,1)}), bf16[128,3072]{1,0:T(8,128)(2,1)}) %reduce-scatter.2.cloned.1.call-update) | async-done | bytes 786448 | tf_op jit(solution)/shard_map/reduce_scatter | solution.py:165
  116.7 7.5 %psum.7 = f32[1,3072]{1,0:T(1,128)} all-reduce(f32[1,3072]{1,0:T(1,128)S(1)} %bitcast.156), channel_id=1, replica_groups=mesh['rep'=16,'tp'=2] {'tp'}, use_global_device_ids=true, to_apply=%region_6.7 | all-reduce | flops 3072 | bytes 24576 | tf_op jit(solution)/shard_map/psum | solution.py:174
  124.2 2.7 %fusion.46 = bf16[1,128,3072]{2,1,0:T(8,128)(2,1)} fusion(bf16[128,3072]{1,0:T(8,128)(2,1)} %reduce-scatter.2.cloned.1.call-done, bf16[1,128,3072]{2,1,0:T(8,128)(2,1)} %param.9, f32[128]{0:T(128)S(1)} %broadcast_multiply_fusion.1, f32[3072]{0:T(1024)S(1)} %bitcast.155, f32[128]{0:T(128)S(1)} %add_rsqrt_fusion), kind=kLoop, calls=%fused_computation.64 | loop fusion | flops 3145728 | bytes 2372608 | tf_op jit(solution)/shard_map/broadcast_in_dim | solution.py:193
  126.9 65.1 %all-gather.6.cloned.1.call-done = f32[1024,3072]{1,0:T(8,128)} async-done(((f32[64,3072]{1,0:T(8,128)}), f32[1024,3072]{1,0:T(8,128)}) %all-gather.6.cloned.1.call-update) | async-done | bytes 12582928 | tf_op jit(solution)/shard_map/all_gather | solution.py:185
  192.1 6.3 %reduce_sum.61 = f32[64,3072]{1,0:T(8,128)} reduce(f32[16,64,3072]{2,1,0:T(8,128)} %bitcast.138, f32[]{:T(128)} %constant.15.clone.1), dimensions={0}, to_apply=%region_8.9 | reduce | flops 2949120 | bytes 13369348 | tf_op jit(solution)/shard_map/reduce_sum | solution.py:185
  198.3 3.0 %multiply_subtract_fusion = (f32[64,3072]{1,0:T(8,128)}, f32[64,3072]{1,0:T(8,128)}) fusion(f32[64,3072]{1,0:T(8,128)} %param.15, f32[64,3072]{1,0:T(8,128)} %reduce_sum.61, f32[64,3072]{1,0:T(8,128)} %param.16), kind=kLoop, calls=%fused_computation.66 | loop fusion | flops 1376256 | bytes 3932160 | tf_op jit(solution)/shard_map/sub | solution.py:187
  (49 shorter events, 17.8 us)
Async XLA Ops:
  8.0 34.0 %copy-start = (bf16[1,3072,512]{2,1,0:T(8,128)(2,1)S(1)}, bf16[1,3072,512]{2,1,0:T(8,128)(2,1)}, u32[]{:S(2)}) copy-start(bf16[1,3072,512]{2,1,0:T(8,128)(2,1)} %param.13) | copy-start | bytes 9437188
  8.0 34.0 %all-gather.4.cloned.1.call-start = ((), (), s32[]{:S(2)}) async-start(), calls=%async_computation.1 | async-start | bytes 2359296 | tf_op jit(solution)/shard_map/all_gather | solution.py:106
  11.9 102.8 %reduce-scatter.2.cloned.1.call-start = ((), (), s32[]{:S(2)}) async-start(), calls=%async_computation.2 | async-start | bytes 2359296 | tf_op jit(solution)/shard_map/reduce_scatter | solution.py:165
  46.8 3.6 %copy-start.1 = (bf16[256,3072]{1,0:T(8,128)(2,1)S(1)}, bf16[256,3072]{1,0:T(8,128)(2,1)}, u32[]{:S(2)}) copy-start(bf16[256,3072]{1,0:T(8,128)(2,1)} %all-gather.4.cloned.1.call-done) | copy-start | bytes 4718596
  55.0 1.0 copy-start.5
  55.0 1.1 copy-start.8
  77.5 1.5 copy-start.4
  80.1 4.9 %copy-start.9 = (f32[256,4,128]{0,2,1:T(8,128)S(1)}, f32[256,4,128]{0,2,1:T(8,128)}, u32[]{:S(2)}) copy-start(f32[256,4,128]{0,2,1:T(8,128)} %get-tuple-element.50) | copy-start | bytes 1572868
  80.2 5.0 %copy-start.3 = (bf16[1,3072,512]{2,1,0:T(8,128)(2,1)S(1)}, bf16[1,3072,512]{2,1,0:T(8,128)(2,1)}, u32[]{:S(2)}) copy-start(bf16[1,3072,512]{2,1,0:T(8,128)(2,1)} %param.12) | copy-start | bytes 9437188
  85.1 1.1 copy-start.6
  88.4 103.6 %all-gather.6.cloned.1.call-start = ((), (), s32[]{:S(2)}) async-start(), calls=%async_computation.3 | async-start | bytes 13369344 | tf_op jit(solution)/shard_map/all_gather | solution.py:185
  90.9 2.0 copy-start.2
  90.9 2.0 copy-start.7
  98.3 16.4 %copy-start.10 = (f32[1,3072]{1,0:T(1,128)S(1)}, f32[1,3072]{1,0:T(1,128)}, u32[]{:S(2)}) copy-start(f32[1,3072]{1,0:T(1,128)} %param.10) | copy-start | bytes 36868
Sparse Core Ops, SparseCore 0:
  12.0 29.8 all-gather.3
  88.6 26.1 reduce-scatter.1
Sparse Core Ops, SparseCore 1:
  91.8 100.2 all-gather.5
